TPU v7x, 32 devices: a whole 2x2x4 slice. The times are simulated.
32 devices in a mesh: sky: 2 (over y), ma: 4 (over z), freq: 2 (over x), pol: 2 (over core).
Axes of the slice: x: 2, y: 2, z: 4, core: 2. Of those that a mesh axis runs over, the one named last changes fastest.
Arguments:
- alm: bfloat16 [2, 2, 1024, 4, 1024], P(None, 'freq', ('ma', 'pol'), None, 'sky'), parts along dimension 4, may hold values from -6 to 6
- beam: bfloat16 [4, 2, 2, 1024, 1024], P('ma', 'freq', None, 'pol'), may hold values from -0.1875 to 0.1875
- m_table: int32 [4], P('ma'), may hold values from 0 to 511, as said below
- chan_mask: int32 [2], P('freq'), may hold values from 0 to 1, as said below
- noise: float32 [2, 1024], P('freq', 'pol'), may hold values from 0.5 to 4
Outputs:
- scaled: bfloat16 [2, 2, 4, 1024, 1024], P(None, 'freq', 'ma', 'pol', 'sky'), parts along dimension 4
- channel_power: float32 [4], P(('sky', 'freq')), parts along dimension 0
There are 2 independent parts, one for each index of `sky`. A program takes and returns all parts, laid end to end along the dimension named above; an argument that names none is the same for every part. Nothing has to cross between parts.
Inputs may be any that keep to these rules, and one draw needn't show every extreme that they name: `m_table`: the 4 values are distinct whole numbers below 512. `chan_mask`: at least one of the 2 channels is usable.
All inputs are finite; a program needn't handle non-finite values.
Results may differ from a plain program's by a relative error of at most 0.00055.
Values may be sent and summed in bfloat16 or wider, within the bound.
A program may use at most 64 MiB of HBM per device.

v0:
```python
import jax
import jax.numpy as jnp
from jax import lax
from jax.sharding import PartitionSpec as P


def on_device(alm, beam, m_table, chan_mask, noise):
    arrived = lax.all_to_all(alm, "ma", split_axis=3, concat_axis=2, tiled=True)
    blocks = arrived.reshape(
        arrived.shape[0],
        arrived.shape[1],
        lax.axis_size("ma"),
        arrived.shape[2] // lax.axis_size("ma"),
        arrived.shape[4],
    )
    joined = lax.all_gather(blocks, "pol", axis=3, tiled=True)
    coeffs_all = joined.reshape(
        joined.shape[0], joined.shape[1], joined.shape[2] * joined.shape[3], joined.shape[4]
    )
    degree = lax.iota(jnp.int32, coeffs_all.shape[2])
    keep_mask = (degree >= m_table[0])[None, None, :, None]
    coeffs = jnp.where(keep_mask, coeffs_all, jnp.zeros((), coeffs_all.dtype))
    response = beam[0]
    real_part = jnp.einsum(
        "fkl,fls->fks", response[:, 0], coeffs[0], preferred_element_type=jnp.float32
    ) - jnp.einsum("fkl,fls->fks", response[:, 1], coeffs[1], preferred_element_type=jnp.float32)
    imag_part = jnp.einsum(
        "fkl,fls->fks", response[:, 0], coeffs[1], preferred_element_type=jnp.float32
    ) + jnp.einsum("fkl,fls->fks", response[:, 1], coeffs[0], preferred_element_type=jnp.float32)
    visibility = jnp.stack([real_part, imag_part])
    weighted = visibility * visibility / noise[None, :, :, None]
    partial_power = jnp.sum(weighted, axis=(0, 2, 3))
    modes_total = jnp.float32(
        lax.axis_size("ma") * noise.shape[1] * lax.axis_size("pol") * visibility.shape[3]
    )
    mask_float = chan_mask.astype(jnp.float32)
    channel_power = lax.psum(partial_power, ("ma", "pol")) / modes_total
    masked_sum, live_count = lax.psum(
        (jnp.sum(mask_float * channel_power), jnp.sum(mask_float)), "freq"
    )
    band_power = masked_sum / live_count
    factor = mask_float / jnp.sqrt(0.5 * channel_power + 0.5 * band_power + 1e-06)
    scaled = visibility * (lax.rsqrt(noise) * factor[:, None])[None, :, :, None]
    return (scaled[:, :, None].astype(jnp.bfloat16), channel_power)


def solution(mesh):
    return jax.shard_map(
        on_device,
        mesh=mesh,
        in_specs=(
            P(None, "freq", ("ma", "pol"), None, "sky"),
            P("ma", "freq", None, "pol", None),
            P("ma"),
            P("freq"),
            P("freq", "pol"),
        ),
        out_specs=(P(None, "freq", "ma", "pol", "sky"), P(("sky", "freq"))),
        check_vma=False,
    )
```

profile of v0, /device:TPU:0, one launch (start us, length us, event | category | flops | bytes accessed | tf_op | source)
XLA Modules:
  0.0 94.6 jit_solution(7890521315917420241)
XLA Ops:
  7.2 0.0 all-gather.3.cloned.1.call-start
  7.2 1.4 %copy.10 = bf16[2,1,128,4,512]{4,2,0,1,3:T(8,128)(2,1)S(1)} copy(bf16[2,1,128,4,512]{4,3,2,1,0:T(4,128)(2,1)} %param.5) | data formatting | bytes 2097152 | tf_op args[0]
  8.6 31.9 %all_to_all.15 = bf16[2,1,128,4,512]{4,2,0,1,3:T(8,128)(2,1)S(1)} all-to-all(bf16[2,1,128,4,512]{4,2,0,1,3:T(8,128)(2,1)S(1)} %copy.10), channel_id=1, replica_groups=mesh['sky'=2,'ma'=4,'freq'=2,'pol'=2] {'ma'}, dimensions={3} | all-to-all | bytes 2097152 | tf_op jit(solution)/shard_map/all_to_all | solution.py:8
  40.5 1.1 %copy.14 = bf16[2,1,128,4,512]{4,2,3,0,1:T(8,128)(2,1)} copy(bf16[2,1,128,4,512]{4,2,0,1,3:T(8,128)(2,1)S(1)} %all_to_all.15) | data formatting | bytes 2097152 | tf_op jit(solution)/shard_map/all_to_all | solution.py:8
  41.6 0.0 all-gather.3.cloned.1.call-update
  42.9 8.5 %all-gather.3.cloned.1.call-done = bf16[2,1,4,256,1,512]{5,3,2,0,4,1:T(8,128)(2,1)} async-done(((bf16[2,1,4,128,1,512]{5,3,2,0,4,1:T(8,128)(2,1)}), bf16[2,1,4,256,1,512]{5,3,2,0,4,1:T(8,128)(2,1)}) %all-gather.3.cloned.1.call-update) | async-done | bytes 2097168 | tf_op jit(solution)/shard_map/all_gather | solution.py:16
  51.5 0.0 copy-start.1
  51.5 2.0 %broadcast_select_fusion = bf16[2,1,1024,512]{3,2,0,1:T(8,128)(2,1)S(1)} fusion(bf16[2,1,1024,512]{3,2,0,1:T(8,128)(2,1)} %bitcast.47, pred[1024]{0:T(1024)(128)(4,1)S(1)} %iota_compare_fusion), kind=kLoop, calls=%fused_computation.5 | loop fusion | flops 1048576 | bytes 4195328 | tf_op jit(solution)/shard_map/jit(_where)/select_n | solution.py:22
  53.4 0.3 copy-done.1
  53.7 0.7 fusion.3
  54.4 0.8 fusion.4
  55.2 0.8 convolution_subtract_fusion
  55.9 0.0 copy-start
  56.0 0.8 convolution_add_fusion
  56.7 0.0 copy-done
  56.7 1.1 %fusion.2 = f32[]{:T(128)} fusion(f32[1,1,512,512]{2,3,1,0:T(8,128)S(1)} %bitcast.45, f32[1,1,512,512]{2,3,1,0:T(8,128)S(1)} %bitcast.43, f32[512]{0:T(512)S(1)} %bitcast.48), kind=kLoop, calls=%fused_computation.4 | loop fusion | flops 2097151 | bytes 2099204 | tf_op jit(solution)/shard_map/reduce_sum | solution.py:32
  57.9 17.7 %psum.21 = f32[1]{0:T(128)} all-reduce(f32[1]{0:T(128)} %bitcast.16), channel_id=1, replica_groups=mesh['sky'=2,'ma'=4,'freq'=2,'pol'=2] {'ma','pol'}, use_global_device_ids=true, to_apply=%region_1.2 | all-reduce | flops 1 | bytes 8 | tf_op jit(solution)/shard_map/psum | solution.py:37
  76.9 6.7 %all-reduce = (f32[]{:T(128)}, f32[]{:T(128)}) all-reduce(f32[]{:T(128)} %bitcast.17, f32[]{:T(128)} %bitcast.18), channel_id=1, replica_groups=mesh['sky'=2,'ma'=4,'freq'=2,'pol'=2] {'freq'}, use_global_device_ids=true, to_apply=%region_2.3 | all-reduce | flops 2 | bytes 16 | tf_op jit(solution)/shard_map/psum | solution.py:38
  85.0 0.3 fusion
  85.3 1.3 %copy.12 = bf16[2,1,1,512,512]{4,3,2,1,0:T(8,128)(2,1)} copy(bf16[2,1,1,512,512]{3,4,2,1,0:T(8,128)(2,1)S(1)} %fusion) | data formatting | bytes 2097152
  (2 shorter events, 0.0 us)
Async XLA Ops:
  7.2 44.3 %all-gather.3.cloned.1.call-start = ((), (), s32[]{:S(2)}) async-start(), calls=%async_computation.1 | async-start | bytes 3145728 | tf_op jit(solution)/shard_map/all_gather | solution.py:16
  51.5 2.2 %copy-start.1 = (bf16[1,1,2,512,1024]{4,3,2,1,0:T(8,128)(2,1)S(1)}, bf16[1,1,2,512,1024]{4,3,2,1,0:T(8,128)(2,1)}, u32[]{:S(2)}) copy-start(bf16[1,1,2,512,1024]{4,3,2,1,0:T(8,128)(2,1)} %param.6) | copy-start | bytes 6291460
  55.9 0.8 copy-start
Sparse Core Ops, SparseCore 0:
  41.7 9.6 all-gather.2
where the time goes:
time: 94.9 us; the launch traced here: 94.6 us
  blocking collectives  56.3 us (59%)
  between operations  19.3 us (20%)
  waiting for transfers between devices  8.54 us (9%)
  local copies, waits for them, and re-layouts  4.09 us (4%)
  other arithmetic  3.39 us (4%)
  matrix products  3.01 us (3%)
    all_to_all x1, blocking collectives, on_device(): arrived = lax.all_to_all(alm, 'ma', split_axis=3, concat_axis=2, tiled=True)  31.9 us
    psum x1, blocking collectives, on_device(): channel_power = lax.psum(partial_power, ('ma', 'pol')) / modes_total  17.7 us
    all_gather x1, waiting for transfers between devices, on_device(): joined = lax.all_gather(blocks, 'pol', axis=3, tiled=True)  8.53 us
    psum x1, blocking collectives, on_device(): lax.psum((jnp.sum(mask_float * channel_power), jnp.sum(mask_float)), 'freq')  6.71 us
    unnamed x6, local copies, waits for them, and re-layouts  3.01 us
    select_n x1, other arithmetic, on_device(): coeffs = jnp.where(keep_mask, coeffs_all, jnp.zeros((), coeffs_all.dtype))  1.96 us
  transfers between devices with their start and end apart: 1, of which 1 were waited for; matrix products, arithmetic and copies ran while one was open for 0% of the time, Pallas kernels for 0%

commit v1 on v0

--- a/solution.py
+++ b/solution.py
@@ -5,7 +5,9 @@
 
 
 def on_device(alm, beam, m_table, chan_mask, noise):
-    arrived = lax.all_to_all(alm, "ma", split_axis=3, concat_axis=2, tiled=True)
+    arrived = jnp.concatenate(
+        lax.all_to_all(jnp.stack(jnp.split(alm, lax.axis_size("ma"), axis=3)), "ma", 0, 0), axis=2
+    )
     blocks = arrived.reshape(
         arrived.shape[0],
         arrived.shape[1],

time: 94.9 us -> 98.4 us (1.037)
  local copies, waits for them, and re-layouts: 4.09 us -> 9.32 us
  other arithmetic: 3.39 us -> 1.79 us
    split x0 -> x1, local copies, waits for them, and re-layouts: none -> 4.66 us  [on_device(): jnp.split(alm, lax.axis_size('ma'), axis=3)]
    select_n x1, other arithmetic: 1.96 us -> 0.22 us  [on_device(): coeffs = jnp.where(keep_mask, coeffs_all, jnp.zeros((), coeffs_all.dtype))]
    all_gather x0 -> x1, local copies, waits for them, and re-layouts: none -> 1.73 us  [on_device(): joined = lax.all_gather(blocks, 'pol', axis=3, tiled=True)]
    all_to_all x1 -> x0, local copies, waits for them, and re-layouts: 1.08 us -> none  [on_device(): arrived = lax.all_to_all(alm, 'ma', split_axis=3, concat_axis=2, tiled=True)]
    unnamed x6 -> x5, local copies, waits for them, and re-layouts: 3.01 us -> 2.69 us
where the time goes in v1:
time: 98.4 us; the launch traced here: 98.1 us
  blocking collectives  56.4 us (57%)
  between operations  19.1 us (19%)
  local copies, waits for them, and re-layouts  9.32 us (9%)
  waiting for transfers between devices  8.54 us (9%)
  matrix products  3.01 us (3%)
  other arithmetic  1.79 us (2%)
    all_to_all x1, blocking collectives, on_device(): lax.all_to_all(jnp.stack(jnp.split(alm, lax.axis_size('ma'), axis=3)), 'm...  32 us
    psum x1, blocking collectives, on_device(): channel_power = lax.psum(partial_power, ('ma', 'pol')) / modes_total  17.7 us
    all_gather x1, waiting for transfers between devices, on_device(): joined = lax.all_gather(blocks, 'pol', axis=3, tiled=True)  8.53 us
    psum x1, blocking collectives, on_device(): lax.psum((jnp.sum(mask_float * channel_power), jnp.sum(mask_float)), 'freq')  6.71 us
    split x1, local copies, waits for them, and re-layouts, on_device(): jnp.split(alm, lax.axis_size('ma'), axis=3)  4.66 us
    unnamed x5, local copies, waits for them, and re-layouts  2.69 us
  transfers between devices with their start and end apart: 1, of which 1 were waited for; matrix products, arithmetic and copies ran while one was open for 0% of the time, Pallas kernels for 0%

profile of v1, /device:TPU:0, one launch (start us, length us, event | category | flops | bytes accessed | tf_op | source)
XLA Modules:
  0.0 98.1 jit_solution(8006794011398437174)
XLA Ops:
  7.2 0.0 all-gather.3.cloned.1.call-start
  7.2 4.7 %fusion.5 = (bf16[2,1,128,1,512]{4,3,2,1,0:T(2,128)(2,1)S(1)}, bf16[2,1,128,1,512]{4,3,2,1,0:T(2,128)(2,1)S(1)}, bf16[2,1,128,1,512]{4,3,2,1,0:T(2,128)(2,1)S(1)}, bf16[2,1,128,1,512]{4,3,2,1,0:T(2,128)(2,1)S(1)}) fusion(bf16[2,1,128,4,512]{4,3,2,1,0:T(4,128)(2,1)} %param.5), kind=kLoop, calls=%fused_computation.21 | loop fusion | bytes 2097152 | tf_op jit(solution)/shard_map/split | solution.py:9
  11.9 0.1 copy_bitcast_fusion.2
  12.0 0.1 copy_bitcast_fusion
  12.1 0.1 pad_maximum_fusion
  12.3 32.0 %all_to_all.5 = bf16[4,2,1,128,1,512]{5,3,1,4,2,0:T(8,128)(2,1)} all-to-all(bf16[4,2,1,128,1,512]{5,3,1,4,2,0:T(8,128)(2,1)S(1)} %pad_maximum_fusion), channel_id=1, replica_groups=mesh['sky'=2,'ma'=4,'freq'=2,'pol'=2] {'ma'}, dimensions={0} | all-to-all | bytes 2097152 | tf_op jit(solution)/shard_map/all_to_all | solution.py:9
  44.3 0.0 all-gather.3.cloned.1.call-update
  45.6 8.5 %all-gather.3.cloned.1.call-done = bf16[2,1,4,256,1,512]{5,3,0,4,1,2:T(8,128)(2,1)} async-done(((bf16[2,1,4,128,1,512]{5,3,0,4,1,2:T(8,128)(2,1)}), bf16[2,1,4,256,1,512]{5,3,0,4,1,2:T(8,128)(2,1)}) %all-gather.3.cloned.1.call-update) | async-done | bytes 2097168 | tf_op jit(solution)/shard_map/all_gather | solution.py:18
  54.1 1.7 %copy.15 = bf16[2,1,4,256,1,512]{5,3,2,0,4,1:T(8,128)(2,1)S(1)} copy(bf16[2,1,4,256,1,512]{5,3,0,4,1,2:T(8,128)(2,1)} %all-gather.3.cloned.1.call-done) | data formatting | bytes 4194304 | tf_op jit(solution)/shard_map/all_gather | solution.py:18
  55.9 0.0 copy-start.1
  55.9 0.2 broadcast_select_fusion
  56.1 1.4 %copy-done.1 = bf16[1,1,2,512,1024]{4,3,2,1,0:T(8,128)(2,1)S(1)} copy-done((bf16[1,1,2,512,1024]{4,3,2,1,0:T(8,128)(2,1)S(1)}, bf16[1,1,2,512,1024]{4,3,2,1,0:T(8,128)(2,1)}, u32[]{:S(2)}) %copy-start.1) | copy-done | bytes 2097176
  57.4 0.8 fusion.3
  58.2 0.8 fusion.4
  59.0 0.8 convolution_subtract_fusion
  59.7 0.0 copy-start
  59.7 0.8 convolution_add_fusion
  60.5 0.0 copy-done
  60.5 1.1 %fusion.2 = f32[]{:T(128)} fusion(f32[1,1,512,512]{2,3,1,0:T(8,128)S(1)} %bitcast.50, f32[1,1,512,512]{2,3,1,0:T(8,128)S(1)} %bitcast.48, f32[512]{0:T(512)S(1)} %bitcast.52), kind=kLoop, calls=%fused_computation.4 | loop fusion | flops 2097151 | bytes 2099204 | tf_op jit(solution)/shard_map/reduce_sum | solution.py:34
  61.6 17.7 %psum.21 = f32[1]{0:T(128)} all-reduce(f32[1]{0:T(128)} %bitcast.19), channel_id=1, replica_groups=mesh['sky'=2,'ma'=4,'freq'=2,'pol'=2] {'ma','pol'}, use_global_device_ids=true, to_apply=%region_1.2 | all-reduce | flops 1 | bytes 8 | tf_op jit(solution)/shard_map/psum | solution.py:39
  80.5 6.7 %all-reduce = (f32[]{:T(128)}, f32[]{:T(128)}) all-reduce(f32[]{:T(128)} %bitcast.20, f32[]{:T(128)} %bitcast.21), channel_id=1, replica_groups=mesh['sky'=2,'ma'=4,'freq'=2,'pol'=2] {'freq'}, use_global_device_ids=true, to_apply=%region_2.3 | all-reduce | flops 2 | bytes 16 | tf_op jit(solution)/shard_map/psum | solution.py:40
  88.5 0.3 fusion
  88.8 1.3 %copy.16 = bf16[2,1,1,512,512]{4,3,2,1,0:T(8,128)(2,1)} copy(bf16[2,1,1,512,512]{3,4,2,1,0:T(8,128)(2,1)S(1)} %fusion) | data formatting | bytes 2097152
  (2 shorter events, 0.0 us)
Async XLA Ops:
  7.2 47.0 %all-gather.3.cloned.1.call-start = ((), (), s32[]{:S(2)}) async-start(), calls=%async_computation.1 | async-start | bytes 3145728 | tf_op jit(solution)/shard_map/all_gather | solution.py:18
  55.9 1.6 %copy-start.1 = (bf16[1,1,2,512,1024]{4,3,2,1,0:T(8,128)(2,1)S(1)}, bf16[1,1,2,512,1024]{4,3,2,1,0:T(8,128)(2,1)}, u32[]{:S(2)}) copy-start(bf16[1,1,2,512,1024]{4,3,2,1,0:T(8,128)(2,1)} %param.6) | copy-start | bytes 6291460
  59.7 0.8 copy-start
Sparse Core Ops, SparseCore 0:
  44.4 9.6 all-gather.2
